TPU v7x, 16 devices: a whole 2x2x2 slice. The times are simulated.
16 devices in a mesh: dp: 4 (over z, y), ep: 4 (over x, core).
Axes of the slice: x: 2, y: 2, z: 2, core: 2. Of those that a mesh axis runs over, the one named last changes fastest.
Arguments:
- tokens: bfloat16 [2048, 2048], P(('dp', 'ep')), parts along dimension 0
- routes: int32 [2048, 6], P(('dp', 'ep')), parts along dimension 0
- w_router: bfloat16 [2048, 64], replicated
- w_one: bfloat16 [64, 2048, 1408], P('ep')
- w_three: bfloat16 [64, 2048, 1408], P('ep')
- w_two: bfloat16 [64, 1408, 2048], P('ep')
Outputs:
- output: bfloat16 [2048, 2048], P(('dp', 'ep')), parts along dimension 0
There are 4 independent parts. A program takes and returns all parts, laid end to end along the dimension named above; an argument that names none is the same for every part.
All inputs are finite; a program needn't handle non-finite values.
Results may differ from a plain program's by a relative error of at most 0.00821994.
Values are sent between devices in bfloat16 or wider.
A program may use at most 1.25 GiB of HBM per device.

v0:
```python
import jax
import jax.numpy as jnp
from jax import lax
from jax.sharding import PartitionSpec as P


def slot_capacity(num_tokens, top_k, num_experts):
    return 8 * ((3 * num_tokens * top_k + 16 * num_experts - 1) // (16 * num_experts))


def route_gates(tokens, routes, w_router):
    logits = jnp.dot(tokens, w_router, preferred_element_type=jnp.float32)
    return jax.nn.softmax(jnp.take_along_axis(logits, routes, axis=1), axis=-1)


def dispatch_plan(routes, num_experts, capacity):
    top_k = routes.shape[1]
    flat_routes = routes.reshape(-1)
    num_pairs = flat_routes.shape[0]
    sort_order = jnp.argsort(flat_routes, stable=True)
    counts = jax.ops.segment_sum(jnp.ones_like(flat_routes), flat_routes, num_segments=num_experts)
    starts = jnp.cumsum(counts) - counts
    slot_ids = starts[:, None] + jnp.arange(capacity, dtype=jnp.int32)[None, :]
    token_at = sort_order[jnp.minimum(slot_ids, num_pairs - 1)] // top_k
    pair_rank = jnp.zeros_like(sort_order).at[sort_order].set(jnp.arange(num_pairs, dtype=sort_order.dtype))
    pair_row = flat_routes * capacity + pair_rank - starts[flat_routes]
    return token_at, pair_row


def expert_mlp(rows, w_one, w_three, w_two):
    gate_pre = jnp.einsum('erd,edf->erf', rows, w_one, preferred_element_type=jnp.float32)
    up_pre = jnp.einsum('erd,edf->erf', rows, w_three, preferred_element_type=jnp.float32)
    hidden = (jax.nn.silu(gate_pre) * up_pre).astype(jnp.bfloat16)
    return jnp.einsum('erf,efd->erd', hidden, w_two, preferred_element_type=jnp.float32).astype(jnp.bfloat16)


def solution(mesh):
    group_size = mesh.shape['ep']
    row_spec = P(('dp', 'ep'), None)
    expert_spec = P('ep', None, None)

    def device_step(tokens, routes, w_router, w_one, w_three, w_two):
        num_tokens, d_model = tokens.shape
        top_k = routes.shape[1]
        num_experts = w_router.shape[1]
        local_experts = w_one.shape[0]
        capacity = slot_capacity(num_tokens, top_k, num_experts)
        gate_vals = route_gates(tokens, routes, w_router)
        token_at, pair_row = dispatch_plan(routes, num_experts, capacity)
        send_rows = tokens[token_at].reshape(num_experts, 1, capacity, d_model)
        recv_rows = lax.all_to_all(send_rows, 'ep', 0, 1, tiled=True)
        out_rows = expert_mlp(recv_rows.reshape(local_experts, group_size * capacity, d_model), w_one, w_three, w_two)
        back_rows = lax.all_to_all(out_rows.reshape(local_experts, group_size, capacity, d_model), 'ep', 1, 0, tiled=True)
        pair_out = back_rows.reshape(num_experts * capacity, d_model)[pair_row].reshape(num_tokens, top_k, d_model)
        return jnp.sum(gate_vals[:, :, None] * pair_out, axis=1).astype(jnp.bfloat16)

    return jax.shard_map(device_step, mesh=mesh, in_specs=(row_spec, row_spec, P(None, None), expert_spec, expert_spec, expert_spec), out_specs=row_spec, check_vma=False)
```

profile of v0, /device:TPU:0, one launch (start us, length us, event | category | flops | bytes accessed | tf_op | source)
XLA Modules:
  0.0 311.9 jit_solution(7367169977811474339)
XLA Ops:
  0.0 0.9 copy.34
  1.0 5.8 %scatter_custom_fusion = s32[64]{0:T(128)S(1)} fusion(s32[768]{0:T(1024)S(1)} %reshape.194, s32[768]{0:T(1024)S(1)} %broadcast.295, s32[]{:T(128)} %constant.15.clone.1), kind=kCustom, calls=%fused_computation.95 | custom fusion | flops 768 | bytes 260 | tf_op jit(solution)/shard_map/scatter-add | solution.py:21
  7.2 4.4 %sort.17 = (s32[768]{0:T(1024)}, s32[768]{0:T(1024)S(1)}) sort(s32[768]{0:T(1024)S(1)} %reshape.194, s32[768]{0:T(1024)S(1)} %iota.13), dimensions={0}, to_apply=%region_2.3 | sort | flops 7680 | bytes 12288 | tf_op jit(solution)/shard_map/jit(argsort)/sort | solution.py:20
  11.7 5.9 %gather_fusion = s32[1536]{0:T(1024)S(1)} fusion(s32[768]{0:T(1024)S(1)} %get-tuple-element.6, s32[2048]{0:T(1024)S(1)} %pad_clamp_fusion.1), kind=kCustom, calls=%fused_computation | custom fusion | bytes 18432 | tf_op jit(solution)/shard_map/gather | solution.py:24
  17.9 7.1 %gather_fusion.1 = bf16[1536,2048]{1,0:T(8,128)(2,1)} fusion(bf16[128,2048]{1,0:T(8,128)(2,1)S(1)} %copy-done, s32[2048]{0:T(1024)S(1)} %pad_clamp_fusion), kind=kCustom, calls=%fused_computation.1 | custom fusion | bytes 12589056 | tf_op jit(solution)/shard_map/gather | solution.py:50
  25.0 75.3 %all_to_all.30 = bf16[64,1,24,2048]{3,2,1,0:T(8,128)(2,1)S(1)} all-to-all(bf16[64,1,24,2048]{3,2,1,0:T(8,128)(2,1)} %bitcast.101), channel_id=1, replica_groups=mesh['dp'=4,'ep'=4] {'ep'}, dimensions={0} | all-to-all | bytes 12582912 | tf_op jit(solution)/shard_map/all_to_all | solution.py:51
  100.3 3.2 %copy.37 = bf16[16,4,1,24,2048]{4,3,1,0,2:T(8,128)(2,1)} copy(bf16[16,4,1,24,2048]{4,3,0,1,2:T(8,128)(2,1)S(1)} %bitcast.102) | data formatting | bytes 12582912 | tf_op jit(solution)/shard_map/all_to_all | solution.py:51
  103.5 36.7 %fusion.15 = f32[16,96,1408]{2,1,0:T(8,128)} fusion(bf16[16,96,2048]{2,1,0:T(8,128)(2,1)} %bitcast.98, bf16[16,2048,1408]{2,1,0:T(8,128)(2,1)} %param.9), kind=kOutput, calls=%fused_computation.104 | convolution fusion | flops 8858370048 | bytes 107216896 | tf_op jit(solution)/shard_map/erd,edf->erf/dot_general | solution.py:31
  140.2 64.8 %convolution_convert_fusion = bf16[16,96,2048]{2,1,0:T(8,128)(2,1)} fusion(bf16[16,1408,2048]{2,1,0:T(8,128)(2,1)} %param.11, f32[16,96,1408]{2,1,0:T(8,128)} %fusion.15, bf16[16,96,2048]{2,1,0:T(8,128)(2,1)} %bitcast.99, bf16[16,2048,1408]{2,1,0:T(8,128)(2,1)} %param.10), kind=kOutput, calls=%fused_computation.8 | convolution fusion | flops 17732861952 | bytes 205783040 | tf_op jit(solution)/shard_map/erf,efd->erd/dot_general | solution.py:34
  204.9 6.6 %copy.38 = bf16[16,4,24,2048]{3,2,0,1:T(8,128)(2,1)} copy(bf16[16,4,24,2048]{3,2,1,0:T(8,128)(2,1)} %bitcast.100) | data formatting | bytes 12582912 | tf_op jit(solution)/shard_map/reshape | solution.py:53
  211.5 5.5 %all-to-all-start.1 = ((bf16[16,4,24,2048]{3,2,0,1:T(8,128)(2,1)}), bf16[16,4,24,2048]{3,2,0,1:T(8,128)(2,1)}, u32[]{:S(2)}, u32[]{:S(2)}) async-start(bf16[16,4,24,2048]{3,2,0,1:T(8,128)(2,1)} %copy.38), calls=%async_computation.1 | async-start | bytes 12582912 | tf_op jit(solution)/shard_map/all_to_all | solution.py:53
  217.8 5.1 %gather_fusion.3 = f32[768]{0:T(1024)S(1)} fusion(f32[128,64]{0,1:T(8,128)S(1)} %fusion.14, s32[768]{0:T(1024)S(1)} %reshape.297), kind=kCustom, calls=%fused_computation.3 | custom fusion | bytes 12288 | tf_op jit(solution)/shard_map/jit(take_along_axis)/gather | solution.py:13
  223.3 3.4 %scatter_custom_fusion.1 = s32[768]{0:T(1024)S(1)} fusion(s32[768]{0:T(1024)S(1)} %compare_select_fusion.10, s32[768]{0:T(1024)S(1)} %iota.14, s32[]{:T(128)} %constant.15.clone.1), kind=kCustom, calls=%fused_computation.93 | custom fusion | bytes 3076 | tf_op jit(solution)/shard_map/scatter | solution.py:25
  226.7 0.7 fusion.13
  227.4 0.7 fusion.12
  228.1 0.7 fusion.10
  228.8 0.7 fusion.11
  229.6 4.5 %fusion.3 = (s32[768]{0:T(1024)S(1)}, s32[768,1]{0,1:T(1,128)S(1)}) fusion(s32[]{:T(128)} %bitcast.68, s32[]{:T(128)} %bitcast.69, s32[]{:T(128)} %bitcast.70, s32[]{:T(128)} %bitcast.71, s32[]{:T(128)} %bitcast.72, s32[]{:T(128)} %bitcast.74, s32[]{:T(128)} %bitcast.73, s32[768,1]{0,1:T(1,128)S(1)} %broadcast_in_dim_reshape.3), kind=kLoop, calls=%fused_computation.92 | loop fusion | flops 11520 | bytes 9244 | tf_op jit(solution)/shard_map/gather | solution.py:26
  234.0 0.6 compare_reduce_fusion.56
  234.6 35.3 %compare_select_fusion.9 = s32[768]{0:T(1024)S(1)} fusion(pred[768]{0:T(1024)(128)(4,1)S(1)} %get-tuple-element.63, pred[768]{0:T(1024)(128)(4,1)S(1)} %get-tuple-element.62, pred[768]{0:T(1024)(128)(4,1)S(1)} %get-tuple-element.61, pred[768]{0:T(1024)(128)(4,1)S(1)} %get-tuple-element.60, pred[768]{0:T(1024)(128)(4,1)S(1)} %get-tuple-element.59, ...), kind=kLoop, calls=%fused_computation.76 | loop fusion | flops 48384 | bytes 56292 | tf_op jit(solution)/shard_map/select_n | solution.py:54
  270.0 17.3 %all-to-all-done.1 = bf16[16,4,24,2048]{3,2,0,1:T(8,128)(2,1)} async-done(((bf16[16,4,24,2048]{3,2,0,1:T(8,128)(2,1)}), bf16[16,4,24,2048]{3,2,0,1:T(8,128)(2,1)}, u32[]{:S(2)}, u32[]{:S(2)}) %all-to-all-start.1) | async-done | bytes 6291488 | tf_op jit(solution)/shard_map/all_to_all | solution.py:53
  287.2 10.8 %gather_fusion.2 = bf16[768,2048]{1,0:T(8,128)(2,1)} fusion(bf16[1536,2048]{1,0:T(8,128)(2,1)} %bitcast.10, s32[1024]{0:T(1024)S(1)} %pad_clamp_fusion.2), kind=kCustom, calls=%fused_computation.2 | custom fusion | bytes 6294528 | tf_op jit(solution)/shard_map/gather | solution.py:54
  298.0 6.5 %reshape.201 = f32[128,6,2048]{2,1,0:T(8,128)} reshape(bf16[768,2048]{1,0:T(8,128)(2,1)} %gather_fusion.2) | data formatting | bytes 9437184 | tf_op jit(solution)/shard_map/convert_element_type | solution.py:55
  304.5 7.4 %multiply_reduce_fusion = bf16[128,2048]{1,0:T(8,128)(2,1)} fusion(f32[128,6,2048]{2,1,0:T(8,128)} %reshape.201, f32[128,6]{1,0:T(8,128)S(1)} %copy.33), kind=kLoop, calls=%fused_computation.7 | loop fusion | flops 2883584 | bytes 6818816 | tf_op jit(solution)/shard_map/reduce_sum | solution.py:55
  (37 shorter events, 2.0 us)
Async XLA Ops:
  0.0 17.9 %copy-start = (bf16[128,2048]{1,0:T(8,128)(2,1)S(1)}, bf16[128,2048]{1,0:T(8,128)(2,1)}, u32[]{:S(2)}) copy-start(bf16[128,2048]{1,0:T(8,128)(2,1)} %param.6) | copy-start | bytes 1572868
  211.5 5.7 %copy-start.2 = (s32[128,6]{0,1:T(8,128)S(1)}, s32[128,6]{0,1:T(8,128)}, u32[]{:S(2)}) copy-start(s32[128,6]{0,1:T(8,128)} %param.7) | copy-start | bytes 9220
  211.5 6.0 %copy-start.1 = (bf16[2048,64]{0,1:T(8,128)(2,1)S(1)}, bf16[2048,64]{0,1:T(8,128)(2,1)}, u32[]{:S(2)}) copy-start(bf16[2048,64]{0,1:T(8,128)(2,1)} %param.8) | copy-start | bytes 786436
  211.5 75.7 %all-to-all-start.1 = ((bf16[16,4,24,2048]{3,2,0,1:T(8,128)(2,1)}), bf16[16,4,24,2048]{3,2,0,1:T(8,128)(2,1)}, u32[]{:S(2)}, u32[]{:S(2)}) async-start(bf16[16,4,24,2048]{3,2,0,1:T(8,128)(2,1)} %copy.38), calls=%async_computation.1 | async-start | bytes 12582912 | tf_op jit(solution)/shard_map/all_to_all | solution.py:53
where the time goes:
time: 313 us; the launch traced here: 312 us
  matrix products  102 us (33%)
  blocking collectives  75.3 us (24%)
  other arithmetic  58.4 us (19%)
  local copies, waits for them, and re-layouts  53.4 us (17%)
  waiting for transfers between devices  17.3 us (6%)
  starting transfers between devices  5.55 us (2%)
    all_to_all x1, blocking collectives, device_step(): recv_rows = lax.all_to_all(send_rows, 'ep', 0, 1, tiled=True)  75.3 us
    dot_general x1, matrix products, expert_mlp(): jnp.einsum('erf,efd->erd', hidden, w_two, preferred_element_type=jnp.floa...  64.8 us
    dot_general x1, matrix products, expert_mlp(): jnp.einsum('erd,edf->erf', rows, w_one, preferred_element_type=jnp.float32)  36.7 us
    select_n x1, other arithmetic, device_step(): back_rows.reshape(num_experts * capacity, d_model)[pair_row]  35.3 us
    all_to_all x1, waiting for transfers between devices, device_step(): lax.all_to_all(out_rows.reshape(local_experts, group_size, capacity, d_mo...  17.3 us
    gather x1, local copies, waits for them, and re-layouts, device_step(): back_rows.reshape(num_experts * capacity, d_model)[pair_row]  10.8 us
    reduce_sum x1, other arithmetic, device_step(): jnp.sum(gate_vals[:, :, None] * pair_out, axis=1).astype(jnp.bfloat16)  7.4 us
    gather x1, local copies, waits for them, and re-layouts, device_step(): send_rows = tokens[token_at].reshape(num_experts, 1, capacity, d_model)  7.09 us
  transfers between devices with their start and end apart: 1, of which 1 were waited for; matrix products, arithmetic and copies ran while one was open for 17% of the time, Pallas kernels for 0%

commit v1 on v0

v1 whole, which is shorter than its diff:
```python
import functools

import jax
import jax.numpy as jnp
from jax import lax
from jax.experimental import pallas as pl
from jax.experimental.pallas import tpu as pltpu

MESH = pl.DeviceIdType.MESH
PAD = 32
CC = 512
RING = 6
RING2 = 8
UNROLL = 4


def layer_kernel(tok_hbm, rou_hbm, wr_hbm, w1_hbm, w3_hbm, w2_hbm, y_hbm,
                 w13, w2r, tok, meta, code, pg, xbuf, hid, obuf, wr, rou,
                 stage, xsend, own, rec_agg, rec_fin, rec_x, ybuf,
                 w13_sem, w2_sem, in_sem, out_sem,
                 tok_ss, tok_rs, meta_ss, meta_rs, ret_ss, ret_rs):
    me = lax.axis_index('ep')
    core = lax.rem(me, 2)
    sib = me + 1 - 2 * core
    far = lax.rem(me + 2, 4)
    diag = far + 1 - 2 * core
    n_tok, d_model = tok_hbm.shape
    n_exp = wr_hbm.shape[1]
    n_loc, _, d_ff = w1_hbm.shape
    n_chunk = d_model // CC
    rows = 4 * PAD
    f32, bf16 = jnp.float32, jnp.bfloat16

    def w1_copy(e, slot):
        return pltpu.make_async_copy(w1_hbm.at[e], w13.at[slot], w13_sem.at[slot])

    def w3_copy(e, slot):
        return pltpu.make_async_copy(w3_hbm.at[e], w13.at[slot], w13_sem.at[slot])

    def w2_copy(q, slot):
        c = lax.div(q, n_loc)
        e = lax.rem(q, n_loc)
        cols = pl.ds(pl.multiple_of(c * CC, CC), CC)
        return pltpu.make_async_copy(w2_hbm.at[e, :, cols], w2r.at[slot], w2_sem.at[slot])

    tok_in = pltpu.make_async_copy(tok_hbm, tok.at[me], in_sem.at[0])
    rou_in = pltpu.make_async_copy(rou_hbm, rou, in_sem.at[1])
    wr_in = pltpu.make_async_copy(wr_hbm, wr, in_sem.at[2])
    tok_in.start()
    rou_in.start()
    wr_in.start()
    for k in range(RING // 2):
        w1_copy(k, 2 * k).start()
        w3_copy(k, 2 * k + 1).start()
    for k in range(RING2):
        w2_copy(k, k).start()

    barrier = pltpu.get_barrier_semaphore()
    for peer in (sib, far):
        pl.semaphore_signal(barrier, inc=1, device_id={'ep': peer}, device_id_type=MESH)
    pl.semaphore_wait(barrier, 2)

    def send(src, dst, ss, rs, peer):
        return pltpu.make_async_remote_copy(src_ref=src, dst_ref=dst, send_sem=ss, recv_sem=rs,
                                            device_id={'ep': peer}, device_id_type=MESH)

    tok_far = send(tok.at[me], tok.at[me], tok_ss.at[0], tok_rs.at[0], far)
    tok_sib = send(tok.at[me], tok.at[me], tok_ss.at[1], tok_rs.at[1], sib)
    tok_fwd = send(tok.at[far], tok.at[far], tok_ss.at[2], tok_rs.at[2], sib)
    meta_far = send(meta.at[me], meta.at[me], meta_ss.at[0], meta_rs.at[0], far)
    meta_sib = send(meta.at[me], meta.at[me], meta_ss.at[1], meta_rs.at[1], sib)
    meta_fwd = send(meta.at[far], meta.at[far], meta_ss.at[2], meta_rs.at[2], sib)
    tok_in.wait()
    tok_far.start()
    tok_sib.start()

    rou_in.wait()
    wr_in.wait()
    lane = lax.broadcasted_iota(jnp.int32, (n_tok, 2 * n_exp), 1)
    named = lane == rou[:, 0:1]
    for j in range(1, rou.shape[1]):
        named = jnp.logical_or(named, lane == rou[:, j:j + 1])
    logits = jnp.dot(tok[me], wr[...], preferred_element_type=f32)
    logits = jnp.concatenate([logits, logits], axis=1)
    top = jnp.max(jnp.where(named, logits, -jnp.inf), axis=1, keepdims=True)
    ex = jnp.exp(jnp.where(named, logits - top, -jnp.inf))
    gates = ex / jnp.sum(ex, axis=1, keepdims=True)
    meta[me] = jnp.transpose(jnp.where(named, gates, -1.0))[:n_exp, :]
    before = (lax.broadcasted_iota(jnp.int32, (n_tok, n_tok), 0)
              < lax.broadcasted_iota(jnp.int32, (n_tok, n_tok), 1)).astype(f32).astype(bf16)
    meta_far.start()
    meta_sib.start()
    tok_far.wait_recv()
    tok_fwd.start()
    meta_far.wait_recv()
    meta_fwd.start()
    tok_sib.wait_recv()
    meta_sib.wait_recv()
    meta_fwd.wait_recv()

    base = pl.multiple_of(me * n_loc, n_loc)
    slot_r = lax.broadcasted_iota(jnp.int32, (n_loc, PAD, n_tok), 1).astype(f32)
    for s in range(4):
        g = meta[s, pl.ds(base, n_loc), :]
        on = g >= 0.0
        rank = jnp.dot(on.astype(f32).astype(bf16), before, preferred_element_type=f32)
        code[:, s * n_tok:(s + 1) * n_tok] = jnp.where(on, rank + float(s * PAD), -1.0)
        rank = jnp.where(on, rank, -1.0)
        w = jnp.where(rank[:, None, :] == slot_r, g[:, None, :], 0.0)
        w = jnp.transpose(w.reshape(n_loc * PAD, n_tok))
        hi = w.astype(bf16)
        w = w - hi.astype(f32)
        mid = w.astype(bf16)
        w = w - mid.astype(f32)
        pg[s, 0:n_tok, :] = hi
        pg[s, n_tok:2 * n_tok, :] = mid
        pg[s, 2 * n_tok:3 * n_tok, :] = w.astype(bf16)
    tok_fwd.wait_recv()

    row_id = lax.broadcasted_iota(jnp.int32, (rows, 4 * n_tok), 0).astype(f32)
    tok_all = tok.reshape(4 * n_tok, d_model)

    def up(e, _):
        pick = jnp.where(code[pl.ds(e, 1), :] == row_id, 1.0, 0.0).astype(bf16)
        for n in range(0, d_model, 512):
            xbuf[:, n:n + 512] = jnp.dot(pick, tok_all[:, n:n + 512], preferred_element_type=f32).astype(bf16)
        s1 = lax.rem(2 * e, RING)
        s3 = lax.rem(2 * e + 1, RING)
        w1_copy(e, s1).wait()
        w3_copy(e, s3).wait()
        for n in range(0, d_ff, 256):
            m = min(n + 256, d_ff)
            a = jnp.dot(xbuf[...], w13[s1, :, n:m], preferred_element_type=f32)
            b = jnp.dot(xbuf[...], w13[s3, :, n:m], preferred_element_type=f32)
            hid[e, :, n:m] = (a / (1.0 + jnp.exp(-a)) * b).astype(bf16)

        @pl.when(e + RING // 2 < n_loc)
        def _():
            w1_copy(e + RING // 2, s1).start()
            w3_copy(e + RING // 2, s3).start()
        return 0

    lax.fori_loop(0, n_loc, up, 0)

    def agg_in(c):
        return send(stage.at[0], rec_agg.at[c], ret_ss.at[0, c], ret_rs.at[0, c], sib)

    def fin_in(c):
        return send(stage.at[1], rec_fin.at[c], ret_ss.at[1, c], ret_rs.at[1, c], sib)

    def x_in(c):
        return send(xsend.at[c], rec_x.at[c], ret_ss.at[2, c], ret_rs.at[2, c], far)

    def forward(c):
        agg_in(c).wait()
        xsend[c] = xsend[c] + rec_agg[c]
        x_in(c).start()
        fin_in(c).wait_send()

    def part(s):
        o = obuf[:, pl.ds(pl.multiple_of(s * PAD, PAD), PAD), :].reshape(n_loc * PAD, CC)
        p = jnp.dot(pg[s], o, preferred_element_type=f32)
        return p[:n_tok] + p[n_tok:2 * n_tok] + p[2 * n_tok:]

    n_q = n_chunk * n_loc

    def down(c, _):
        def some(i, _):
            for k in range(UNROLL):
                e = i * UNROLL + k
                q = c * n_loc + e
                w2_copy(q, lax.rem(q, RING2)).wait()
            for k in range(UNROLL):
                e = i * UNROLL + k
                q = c * n_loc + e
                obuf[e] = jnp.dot(hid[e], w2r[lax.rem(q, RING2)], preferred_element_type=f32).astype(bf16)
            for k in range(UNROLL):
                q = c * n_loc + i * UNROLL + k

                @pl.when(q + RING2 < n_q)
                def _():
                    w2_copy(q + RING2, lax.rem(q, RING2)).start()
            return 0

        lax.fori_loop(0, n_loc // UNROLL, some, 0)

        @pl.when(c > 0)
        def _():
            forward(c - 1)
        stage[0] = part(diag)
        stage[1] = part(sib)
        agg_in(c).start()
        fin_in(c).start()
        xsend[c] = part(far)
        own[c] = part(me)
        return 0

    lax.fori_loop(0, n_chunk, down, 0)
    forward(n_chunk - 1)

    for c in range(n_chunk):
        fin_in(c).wait_recv()
        x_in(c).wait_recv()
        ybuf[:, c * CC:(c + 1) * CC] = (own[c] + rec_fin[c] + rec_x[c]).astype(bf16)
    y_out = pltpu.make_async_copy(ybuf, y_hbm, out_sem.at[0])
    y_out.start()
    for c in range(n_chunk):
        x_in(c).wait_send()
    for copy in (tok_far, tok_sib, tok_fwd, meta_far, meta_sib, meta_fwd):
        copy.wait_send()
    y_out.wait()


def solution(mesh):
    row_spec = jax.sharding.PartitionSpec(('dp', 'ep'), None)
    expert_spec = jax.sharding.PartitionSpec('ep', None, None)

    def device_step(tokens, routes, w_router, w_one, w_three, w_two):
        n_tok, d_model = tokens.shape
        n_loc, _, d_ff = w_one.shape
        n_exp = w_router.shape[1]
        n_chunk = d_model // CC
        any_spec = pl.BlockSpec(memory_space=pl.ANY)
        f32, bf16 = jnp.float32, jnp.bfloat16
        flops = 2 * n_loc * 4 * PAD * d_model * d_ff * 3
        return pl.pallas_call(
            layer_kernel,
            out_shape=jax.ShapeDtypeStruct((n_tok, d_model), bf16),
            in_specs=[any_spec] * 6,
            out_specs=any_spec,
            scratch_shapes=[
                pltpu.VMEM((RING, d_model, d_ff), bf16),
                pltpu.VMEM((RING2, d_ff, CC), bf16),
                pltpu.VMEM((4, n_tok, d_model), bf16),
                pltpu.VMEM((4, n_exp, n_tok), f32),
                pltpu.VMEM((n_loc, 4 * n_tok), f32),
                pltpu.VMEM((4, 3 * n_tok, n_loc * PAD), bf16),
                pltpu.VMEM((4 * PAD, d_model), bf16),
                pltpu.VMEM((n_loc, 4 * PAD, d_ff), bf16),
                pltpu.VMEM((n_loc, 4 * PAD, CC), bf16),
                pltpu.VMEM(w_router.shape, bf16),
                pltpu.VMEM(routes.shape, jnp.int32),
                pltpu.VMEM((2, n_tok, CC), f32),
                pltpu.VMEM((n_chunk, n_tok, CC), f32),
                pltpu.VMEM((n_chunk, n_tok, CC), f32),
                pltpu.VMEM((n_chunk, n_tok, CC), f32),
                pltpu.VMEM((n_chunk, n_tok, CC), f32),
                pltpu.VMEM((n_chunk, n_tok, CC), f32),
                pltpu.VMEM((n_tok, d_model), bf16),
                pltpu.SemaphoreType.DMA((RING,)),
                pltpu.SemaphoreType.DMA((RING2,)),
                pltpu.SemaphoreType.DMA((3,)),
                pltpu.SemaphoreType.DMA((1,)),
                pltpu.SemaphoreType.DMA((3,)),
                pltpu.SemaphoreType.DMA((3,)),
                pltpu.SemaphoreType.DMA((3,)),
                pltpu.SemaphoreType.DMA((3,)),
                pltpu.SemaphoreType.DMA((3, n_chunk)),
                pltpu.SemaphoreType.DMA((3, n_chunk)),
            ],
            compiler_params=pltpu.CompilerParams(collective_id=0, has_side_effects=True,
                                                 vmem_limit_bytes=67043328),
            cost_estimate=pl.CostEstimate(flops=flops, bytes_accessed=2 * n_loc * d_model * d_ff * 3, transcendentals=0),
        )(tokens, routes, w_router, w_one, w_three, w_two)

    return jax.shard_map(device_step, mesh=mesh, in_specs=(row_spec, row_spec, jax.sharding.PartitionSpec(None, None),
                                                           expert_spec, expert_spec, expert_spec),
                         out_specs=row_spec, check_vma=False)
```

time: 313 us -> 123 us (0.39)
  Pallas kernels: 0 us -> 118 us
  matrix products: 102 us -> 0 us
  blocking collectives: 75.3 us -> 0 us
  other arithmetic: 58.4 us -> 0 us
  local copies, waits for them, and re-layouts: 53.4 us -> 5.25 us
  waiting for transfers between devices: 17.3 us -> 0 us
  starting transfers between devices: 5.55 us -> 0 us
    pallas_call x0 -> x1, Pallas kernels: none -> 118 us  [device_step(): pl.pallas_call(layer_kernel, out_shape=jax.ShapeDtypeStruct((n_tok, d_mod...]
    dot_general x3 -> x0, matrix products: 102 us -> none  [the longest x1 64.8 us: expert_mlp(): jnp.einsum('erf,efd->erd', hidden, w_two, preferred_element_type=jnp.floa...]
    all_to_all x1 -> x0, blocking collectives: 75.3 us -> none  [device_step(): recv_rows = lax.all_to_all(send_rows, 'ep', 0, 1, tiled=True)]
    select_n x4 -> x0, other arithmetic: 35.4 us -> none  [the longest x1 35.3 us: device_step(): back_rows.reshape(num_experts * capacity, d_model)[pair_row]]
    gather x12 -> x0, local copies, waits for them, and re-layouts: 32.1 us -> none  [the longest x1 10.8 us: device_step(): back_rows.reshape(num_experts * capacity, d_model)[pair_row]]
    all_to_all x1 -> x0, waiting for transfers between devices: 17.3 us -> none  [device_step(): lax.all_to_all(out_rows.reshape(local_experts, group_size, capacity, d_mo...]
    reduce_sum x2 -> x0, other arithmetic: 7.42 us -> none  [the longest x1 7.4 us: device_step(): jnp.sum(gate_vals[:, :, None] * pair_out, axis=1).astype(jnp.bfloat16)]
    reshape x2 -> x0, local copies, waits for them, and re-layouts: 6.7 us -> none  [the longest x1 6.56 us: device_step(): out_rows.reshape(local_experts, group_size, capacity, d_model)]
  transfers between devices with their start and end apart: 1 -> 0, of which waited for: 1 -> 0; matrix products, arithmetic and copies ran while one was open for 17% -> 0% of each run, Pallas kernels for 0% -> 0%
where the time goes in v1:
time: 123 us
  Pallas kernels  118 us (96%)
  local copies, waits for them, and re-layouts  5.25 us (4%)
    pallas_call x1, Pallas kernels, device_step(): pl.pallas_call(layer_kernel, out_shape=jax.ShapeDtypeStruct((n_tok, d_mod...  118 us
    unnamed x3, local copies, waits for them, and re-layouts  5.25 us

profile of v1, /device:TPU:0, one launch (start us, length us, event | category | flops | bytes accessed | tf_op | source)
XLA Modules:
  0.0 122.8 jit_solution(13408730494063125021)
XLA Ops:
  0.0 1.4 %copy.7.rou_hbm = s32[128,6]{1,0:T(8,128)} copy(s32[128,6]{0,1:T(8,128)} %param.7) | data formatting | bytes 6144 | tf_op args[1]
  1.4 2.0 %copy.8.wr_hbm = bf16[2048,64]{1,0:T(8,128)(2,1)} copy(bf16[2048,64]{0,1:T(8,128)(2,1)} %param.8) | data formatting | bytes 524288 | tf_op args[2]
  3.4 117.6 %shard_map.64 = bf16[128,2048]{1,0:T(8,128)(2,1)} custom-call(bf16[128,2048]{1,0:T(8,128)(2,1)} %tok_hbm.1, s32[128,6]{1,0:T(8,128)} %copy.7.rou_hbm, bf16[2048,64]{1,0:T(8,128)(2,1)} %copy.8.wr_hbm, bf16[16,2048,1408]{2,1,0:T(8,128)(2,1)} %w1_hbm.1, bf16[16,2048,1408]{2,1,0:T(8,128)(2,1)} %w3_hbm.1, bf16[16,1408,2048]{2,1,0:T(8,128)(2,1)} %w2_hbm.1), custom_call_target="tpu_custom_call" | custom-call | flops 35433480192 | bytes 276824064 | tf_op jit(solution)/shard_map/pallas_call | solution.py:226
  121.0 1.9 %copy.10 = bf16[128,2048]{1,0:T(8,128)(2,1)} copy(bf16[128,2048]{1,0:T(8,128)(2,1)} %shard_map.64) | data formatting | bytes 1048576

commit v2 on v1

--- a/solution.py
+++ b/solution.py
@@ -25,7 +25,7 @@
     far = lax.rem(me + 2, 4)
     diag = far + 1 - 2 * core
     n_tok, d_model = tok_hbm.shape
-    n_exp = wr_hbm.shape[1]
+    n_exp = wr_hbm.shape[0]
     n_loc, _, d_ff = w1_hbm.shape
     n_chunk = d_model // CC
     rows = 4 * PAD
@@ -49,6 +49,9 @@
     tok_in.start()
     rou_in.start()
     wr_in.start()
+    tok_in.wait()
+    rou_in.wait()
+    wr_in.wait()
     for k in range(RING // 2):
         w1_copy(k, 2 * k).start()
         w3_copy(k, 2 * k + 1).start()
@@ -70,22 +73,18 @@
     meta_far = send(meta.at[me], meta.at[me], meta_ss.at[0], meta_rs.at[0], far)
     meta_sib = send(meta.at[me], meta.at[me], meta_ss.at[1], meta_rs.at[1], sib)
     meta_fwd = send(meta.at[far], meta.at[far], meta_ss.at[2], meta_rs.at[2], sib)
-    tok_in.wait()
     tok_far.start()
     tok_sib.start()
 
-    rou_in.wait()
-    wr_in.wait()
-    lane = lax.broadcasted_iota(jnp.int32, (n_tok, 2 * n_exp), 1)
-    named = lane == rou[:, 0:1]
-    for j in range(1, rou.shape[1]):
-        named = jnp.logical_or(named, lane == rou[:, j:j + 1])
-    logits = jnp.dot(tok[me], wr[...], preferred_element_type=f32)
-    logits = jnp.concatenate([logits, logits], axis=1)
-    top = jnp.max(jnp.where(named, logits, -jnp.inf), axis=1, keepdims=True)
+    expert = lax.broadcasted_iota(jnp.int32, (n_exp, n_tok), 0)
+    named = expert == rou[0:1, :]
+    for j in range(1, rou.shape[0]):
+        named = jnp.logical_or(named, expert == rou[j:j + 1, :])
+    logits = lax.dot_general(wr[...], tok[me], (((1,), (1,)), ((), ())), preferred_element_type=f32)
+    top = jnp.max(jnp.where(named, logits, -jnp.inf), axis=0, keepdims=True)
     ex = jnp.exp(jnp.where(named, logits - top, -jnp.inf))
-    gates = ex / jnp.sum(ex, axis=1, keepdims=True)
-    meta[me] = jnp.transpose(jnp.where(named, gates, -1.0))[:n_exp, :]
+    gates = ex / jnp.sum(ex, axis=0, keepdims=True)
+    meta[me] = jnp.where(named, gates, -1.0)
     before = (lax.broadcasted_iota(jnp.int32, (n_tok, n_tok), 0)
               < lax.broadcasted_iota(jnp.int32, (n_tok, n_tok), 1)).astype(f32).astype(bf16)
     meta_far.start()
@@ -182,11 +181,13 @@
                     w2_copy(q + RING2, lax.rem(q, RING2)).start()
             return 0
 
-        lax.fori_loop(0, n_loc // UNROLL, some, 0)
+        some(0, 0)
 
         @pl.when(c > 0)
         def _():
             forward(c - 1)
+        lax.fori_loop(1, n_loc // UNROLL, some, 0)
+
         stage[0] = part(diag)
         stage[1] = part(sib)
         agg_in(c).start()
@@ -238,8 +239,8 @@
                 pltpu.VMEM((4 * PAD, d_model), bf16),
                 pltpu.VMEM((n_loc, 4 * PAD, d_ff), bf16),
                 pltpu.VMEM((n_loc, 4 * PAD, CC), bf16),
-                pltpu.VMEM(w_router.shape, bf16),
-                pltpu.VMEM(routes.shape, jnp.int32),
+                pltpu.VMEM((n_exp, d_model), bf16),
+                pltpu.VMEM(routes.shape[::-1], jnp.int32),
                 pltpu.VMEM((2, n_tok, CC), f32),
                 pltpu.VMEM((n_chunk, n_tok, CC), f32),
                 pltpu.VMEM((n_chunk, n_tok, CC), f32),
@@ -261,7 +262,7 @@
             compiler_params=pltpu.CompilerParams(collective_id=0, has_side_effects=True,
                                                  vmem_limit_bytes=67043328),
             cost_estimate=pl.CostEstimate(flops=flops, bytes_accessed=2 * n_loc * d_model * d_ff * 3, transcendentals=0),
-        )(tokens, routes, w_router, w_one, w_three, w_two)
+        )(tokens, routes.T, w_router.T, w_one, w_three, w_two)
 
     return jax.shard_map(device_step, mesh=mesh, in_specs=(row_spec, row_spec, jax.sharding.PartitionSpec(None, None),
                                                            expert_spec, expert_spec, expert_spec),

time: 123 us -> 110 us (0.89)
  Pallas kernels: 118 us -> 107 us
  local copies, waits for them, and re-layouts: 5.25 us -> 1.88 us
    pallas_call x1, Pallas kernels: 118 us -> 107 us  [device_step(): pl.pallas_call(layer_kernel, out_shape=jax.ShapeDtypeStruct((n_tok, d_mod...]
    unnamed x3 -> x1, local copies, waits for them, and re-layouts: 5.25 us -> 1.88 us
where the time goes in v2:
time: 110 us; the launch traced here: 109 us
  Pallas kernels  107 us (97%)
  local copies, waits for them, and re-layouts  1.88 us (2%)
    pallas_call x1, Pallas kernels, device_step(): pl.pallas_call(layer_kernel, out_shape=jax.ShapeDtypeStruct((n_tok, d_mod...  107 us

profile of v2, /device:TPU:0, one launch (start us, length us, event | category | flops | bytes accessed | tf_op | source)
XLA Modules:
  0.0 109.3 jit_solution(16260846467734732521)
XLA Ops:
  0.0 107.5 %shard_map.64 = bf16[128,2048]{1,0:T(8,128)(2,1)} custom-call(bf16[128,2048]{1,0:T(8,128)(2,1)} %tok_hbm.1, s32[6,128]{1,0:T(8,128)} %bitcast.3, bf16[64,2048]{1,0:T(8,128)(2,1)} %bitcast.2, bf16[16,2048,1408]{2,1,0:T(8,128)(2,1)} %w1_hbm.1, bf16[16,2048,1408]{2,1,0:T(8,128)(2,1)} %w3_hbm.1, bf16[16,1408,2048]{2,1,0:T(8,128)(2,1)} %w2_hbm.1), custom_call_target="tpu_custom_call" | custom-call | flops 35433480192 | bytes 276824064 | tf_op jit(solution)/shard_map/pallas_call | solution.py:227
  107.5 1.9 %copy.8 = bf16[128,2048]{1,0:T(8,128)(2,1)} copy(bf16[128,2048]{1,0:T(8,128)(2,1)} %shard_map.64) | data formatting | bytes 1048576
